TPU v7x, 256 devices: a whole 4x4x8 slice. The times are simulated.
256 devices in a mesh: row: 16 (over z_lo, x, core), col: 16 (over y, z_hi).
Axes of the slice: x: 4, y: 4, z: 8 (z_hi: 4, z_lo: 2; z = z_hi * 2 + z_lo), core: 2. Of those that a mesh axis runs over, the one named last changes fastest.
Arguments:
- object_slices: float32 [4, 2, 4096, 4096], P(None, None, 'row', 'col'), may hold values from -2.5 to 2.5
- probe_wave: float32 [2, 128, 128], replicated, may hold values from -4 to 4
- offsets: int32 [16, 16, 4, 2], P('row', 'col'), may hold values from 0 to 255
- active_flags: int32 [16, 16, 4], P('row', 'col'), may hold values 0 or 1
- intensity: float32 [16, 16, 4, 128, 128], P('row', 'col'), may hold values from 0.1 to 3
Outputs:
- updated_object: float32 [4, 2, 4096, 4096], P(None, None, 'row', 'col')
- updated_probe: float32 [2, 128, 128], replicated
Inputs may be any that keep to these rules, and one draw needn't show every extreme that they name: `offsets`: each position's centre lies in its own device's tile; its window may reach into neighbouring tiles, diagonal ones included. `active_flags`: positions with flag 0 contribute nothing.
All inputs are finite; a program needn't handle non-finite values. No bound on the sum of `active_flags` on one device may be relied on, other than what follows from the above.
Results may differ from a plain program's by a relative error of at most 0.00018.
Values sent between devices are 32-bit elements; how exact they have to be, the bound alone decides.
A program may use at most 64 MiB of HBM per device.

v0:
```python
import math

import jax
import jax.numpy as jnp
from jax import lax
from jax.sharding import PartitionSpec as P

fresnel_phase = 40.0
object_step = 0.25
exact = lax.Precision.HIGHEST


def padded_2(cells, sides, width):
    for axis, dim in sides:
        count = lax.axis_size(axis)
        head = lax.slice_in_dim(cells, 0, width, axis=dim)
        tail = lax.slice_in_dim(cells, cells.shape[dim] - width, cells.shape[dim], axis=dim)
        cells = jnp.concatenate(
            [
                lax.ppermute(tail, axis, [(i, (i + 1) % count) for i in range(count)]),
                cells,
                lax.ppermute(head, axis, [((i + 1) % count, i) for i in range(count)]),
            ],
            axis=dim,
        )
    return cells


def passed_along(array, axis, by):
    length = lax.axis_size(axis)
    return lax.ppermute(array, axis, [(i, (i + by) % length) for i in range(length)])


def dft_tables(extent):
    indices = jnp.arange(extent, dtype=jnp.int32)
    angles = (indices[:, None] * indices[None, :] % extent).astype(jnp.float32) * (
        2.0 * jnp.pi / extent
    )
    norming = 1.0 / math.sqrt(extent)
    cosine = jnp.cos(angles) * norming
    sine_part = -jnp.sin(angles) * norming
    forward = jnp.stack([jnp.stack([cosine, -sine_part]), jnp.stack([sine_part, cosine])])
    backward = jnp.stack([jnp.stack([cosine, sine_part]), jnp.stack([-sine_part, cosine])])
    return (forward, backward)


def transfer(extent):
    indices = jnp.arange(extent, dtype=jnp.int32)
    frequency = ((indices + extent // 2) % extent - extent // 2).astype(jnp.float32) / extent
    phase_angle = -jnp.pi * fresnel_phase * (frequency[:, None] ** 2 + frequency[None, :] ** 2)
    return (jnp.cos(phase_angle), jnp.sin(phase_angle))


def transform(field_pair, tables, inverse):
    block = tables[1] if inverse else tables[0]
    stacked = jnp.stack(field_pair)
    left = jnp.einsum("pqjk,qbkl->pbjl", block, stacked, precision=exact)
    result = jnp.einsum("qbjk,pqkl->pbjl", left, block, precision=exact)
    return (result[0], result[1])


def complex_times(first, second):
    return (
        first[0] * second[0] - first[1] * second[1],
        first[0] * second[1] + first[1] * second[0],
    )


def conj_times(first, second):
    return (
        first[0] * second[0] + first[1] * second[1],
        first[0] * second[1] - first[1] * second[0],
    )


def propagate(field_pair, tables, kernel, adjoint):
    spectrum = transform(field_pair, tables, False)
    if adjoint:
        spectrum = conj_times(kernel, spectrum)
    else:
        spectrum = complex_times(kernel, spectrum)
    return transform(spectrum, tables, True)


def fetch_rim(object_slices, margin):
    return padded_2(object_slices, (("row", 2), ("col", 3)), margin)


def body(object_slices, probe_wave, offsets, active_flags, intensity):
    extent = probe_wave.shape[-1]
    margin = extent // 2
    layers = object_slices.shape[0]
    positions = offsets.shape[2]
    padded = fetch_rim(object_slices, margin)
    start_rows = offsets[0, 0, :, 0]
    start_cols = offsets[0, 0, :, 1]
    anchor = jnp.zeros((), jnp.int32)

    def window_at(source, top_row, left_col):
        return lax.dynamic_slice(
            source, (anchor, anchor, top_row, left_col), (layers, 2, extent, extent)
        )

    windows = jax.vmap(window_at, in_axes=(None, 0, 0))(padded, start_rows, start_cols)
    tables = dft_tables(extent)
    kernel = transfer(extent)
    flags = active_flags[0, 0].astype(jnp.float32)[:, None, None]
    observed = intensity[0, 0]
    wavefield = (
        jnp.broadcast_to(probe_wave[0], (positions, extent, extent)),
        jnp.broadcast_to(probe_wave[1], (positions, extent, extent)),
    )
    incident = []
    for layer_at in range(layers):
        incident.append(wavefield)
        transmit = (windows[:, layer_at, 0], windows[:, layer_at, 1])
        wavefield = complex_times(wavefield, transmit)
        if layer_at + 1 < layers:
            wavefield = propagate(wavefield, tables, kernel, False)
    far_field = transform(wavefield, tables, False)
    excess = flags * (far_field[0] ** 2 + far_field[1] ** 2 - observed)
    back_field = transform((excess * far_field[0], excess * far_field[1]), tables, True)
    grad_layers = [None] * layers
    for layer_at in reversed(range(layers)):
        transmit = (windows[:, layer_at, 0], windows[:, layer_at, 1])
        grad_layers[layer_at] = conj_times(incident[layer_at], back_field)
        back_field = conj_times(transmit, back_field)
        if layer_at > 0:
            back_field = propagate(back_field, tables, kernel, True)
    stacked = jnp.stack([jnp.stack(grad_pair, axis=1) for grad_pair in grad_layers], axis=1)

    def deposit(index_k, running):
        begin = (anchor, anchor, start_rows[index_k], start_cols[index_k])
        piece = stacked[index_k]
        return lax.dynamic_update_slice(
            running, lax.dynamic_slice(running, begin, piece.shape) + piece, begin
        )

    grad_pad = lax.fori_loop(0, positions, deposit, jnp.zeros_like(padded))
    from_right = passed_along(grad_pad[:, :, :, :margin], "col", -1)
    from_left = passed_along(grad_pad[:, :, :, -margin:], "col", 1)
    inner = grad_pad[:, :, :, margin:-margin]
    inner = inner.at[:, :, :, -margin:].add(from_right)
    inner = inner.at[:, :, :, :margin].add(from_left)
    from_below = passed_along(inner[:, :, :margin], "row", -1)
    from_above = passed_along(inner[:, :, -margin:], "row", 1)
    folded = inner[:, :, margin:-margin]
    folded = folded.at[:, :, -margin:].add(from_below)
    folded = folded.at[:, :, :margin].add(from_above)
    updated_object = object_slices - object_step * folded
    local_grad = jnp.stack([jnp.sum(back_field[0], axis=0), jnp.sum(back_field[1], axis=0)])
    devices = lax.axis_size("row") * lax.axis_size("col")
    factor = 1.0 / math.sqrt(positions * devices)
    summed = lax.psum(local_grad, ("row", "col"))
    updated_probe = probe_wave - factor * summed
    return (updated_object, updated_probe)


def solution(mesh):
    in_specs = (
        P(None, None, "row", "col"),
        P(),
        P("row", "col", None, None),
        P("row", "col", None),
        P("row", "col", None, None, None),
    )
    out_specs = (P(None, None, "row", "col"), P())
    return jax.shard_map(body, mesh=mesh, in_specs=in_specs, out_specs=out_specs, check_vma=False)
```

profile of v0, /device:TPU:1, one launch (start us, length us, event | category | flops | bytes accessed | tf_op | source)
XLA Modules:
  0.0 510.7 jit_solution(18418235282657406992)
XLA Ops:
  7.2 2.3 fusion.89
  9.5 2.6 collective-permute-start
  12.7 2.0 copy.120
  15.9 2.6 collective-permute-done
  18.5 2.4 copy.52
  21.3 2.3 copy.54
  23.7 1.9 pad_maximum_fusion.4
  25.6 3.1 collective-permute-start.2
  28.7 5.6 %collective-permute-start.3 = (f32[4,2,384,64]{2,3,1,0:T(8,128)S(1)}, f32[4,2,384,64]{2,3,1,0:T(8,128)S(1)}, u32[]{:S(2)}, u32[]{:S(2)}) collective-permute-start(f32[4,2,384,64]{2,3,1,0:T(8,128)S(1)} %get-tuple-element.205), channel_id=1, source_target_pairs={{1,0},{2,1},{3,2},{4,3},{5,4},{6,5},{7,6},{8,7},{9,8},{10,9},{11,1... | collective-permute-start | bytes 2359304 | tf_op jit(solution)/shard_map/ppermute | solution.py:22
  34.6 20.8 %collective-permute-done.2 = f32[4,2,384,64]{2,3,1,0:T(8,128)S(1)} collective-permute-done((f32[4,2,384,64]{2,3,1,0:T(8,128)S(1)}, f32[4,2,384,64]{2,3,1,0:T(8,128)S(1)}, u32[]{:S(2)}, u32[]{:S(2)}) %collective-permute-start.2) | collective-permute-done | bytes 786464 | tf_op jit(solution)/shard_map/ppermute | solution.py:20
  55.4 11.8 %collective-permute-done.3 = f32[4,2,384,64]{2,3,1,0:T(8,128)S(1)} collective-permute-done((f32[4,2,384,64]{2,3,1,0:T(8,128)S(1)}, f32[4,2,384,64]{2,3,1,0:T(8,128)S(1)}, u32[]{:S(2)}, u32[]{:S(2)}) %collective-permute-start.3) | collective-permute-done | bytes 786464 | tf_op jit(solution)/shard_map/ppermute | solution.py:22
  67.2 3.2 pad_maximum_fusion
  70.4 18.9 %while.19 = (s32[]{:T(128)}, f32[4,2,384,384]{2,3,1,0:T(8,128)}, s32[4,4]{1,0:T(4,128)S(1)}, f32[4,4,2,128,128]{3,4,0,2,1:T(8,128)}, s32[]{:T(128)}) while((s32[]{:T(128)}, f32[4,2,384,384]{2,3,1,0:T(8,128)}, s32[4,4]{1,0:T(4,128)S(1)}, f32[4,4,2,128,128]{3,4,0,2,1:T(8,128)}, s32[]{:T(128)}) %tuple.107), condition=%wide.while_cond.4, body=%wide.while_body.4.sunk | while | flops 2 | bytes 4194437 | solution.py:100
  70.4 0.7 fusion.105
  71.1 2.8 constant_dynamic-slice_fusion.11
  74.2 0.9 constant_dynamic-update-slice_fusion.2
  75.1 0.7 fusion.105
  75.8 2.8 constant_dynamic-slice_fusion.11
  79.0 0.9 constant_dynamic-update-slice_fusion.2
  80.5 2.8 constant_dynamic-slice_fusion.11
  83.7 0.8 constant_dynamic-update-slice_fusion.2
  85.2 2.8 constant_dynamic-slice_fusion.11
  88.4 0.9 constant_dynamic-update-slice_fusion.2
  89.3 1.1 fusion.49
  102.0 0.9 convolution_bitcast_fusion.10
  110.6 1.5 pad_maximum_fusion.1
  112.1 2.5 broadcast_in_dim.10.clone
  114.6 63.5 %while.18 = (s32[]{:T(128)}, f32[4,2,384,384]{2,3,1,0:T(8,128)}, s32[4]{0:T(128)S(1)}, s32[4]{0:T(128)S(1)}, f32[4,4,2,128,128]{3,4,0,2,1:T(8,128)}, /*index=5*/s32[]{:T(128)}, s32[]{:T(128)}, s32[]{:T(128)}) while((s32[]{:T(128)}, f32[4,2,384,384]{2,3,1,0:T(8,128)}, s32[4]{0:T(128)S(1)}, s32[4]{0:T(128)S(1)}, ...), condition=%wide.region_1.2_spmd, body=%wide.region_0.1_spmd.sunk | while | flops 131080 | bytes 7864521 | solution.py:139
  119.6 1.1 constant_dynamic-slice_fusion.9
  120.9 1.5 constant_dynamic-slice_fusion.8
  122.9 7.6 %dynamic_update_slice.8 = f32[4,2,384,384]{2,3,1,0:T(8,128)} dynamic-update-slice(f32[4,2,384,384]{2,3,1,0:T(8,128)} %get-tuple-element.352, f32[4,2,128,128]{2,3,1,0:T(8,128)S(1)} %copy.304, s32[]{:T(128)} %constant.169.clone.1..sunk, s32[]{:T(128)} %constant.169.clone.1..sunk, s32[]{:T(128)S(6)} %select_n.167, s32[]{:T(128)S(6)} %select_n.168) | dynamic-update-slice | bytes 1048580 | tf_op jit(solution)/shard_map/while/body/eval_jaxpr/dynamic_update_slice | solution.py:135
  135.5 1.1 constant_dynamic-slice_fusion.9
  136.8 1.5 constant_dynamic-slice_fusion.8
  138.8 7.2 %dynamic_update_slice.8 = f32[4,2,384,384]{2,3,1,0:T(8,128)} dynamic-update-slice(f32[4,2,384,384]{2,3,1,0:T(8,128)} %get-tuple-element.352, f32[4,2,128,128]{2,3,1,0:T(8,128)S(1)} %copy.304, s32[]{:T(128)} %constant.169.clone.1..sunk, s32[]{:T(128)} %constant.169.clone.1..sunk, s32[]{:T(128)S(6)} %select_n.167, s32[]{:T(128)S(6)} %select_n.168) | dynamic-update-slice | bytes 1048580 | tf_op jit(solution)/shard_map/while/body/eval_jaxpr/dynamic_update_slice | solution.py:135
  151.0 1.1 constant_dynamic-slice_fusion.9
  152.3 1.5 constant_dynamic-slice_fusion.8
  154.3 7.8 %dynamic_update_slice.8 = f32[4,2,384,384]{2,3,1,0:T(8,128)} dynamic-update-slice(f32[4,2,384,384]{2,3,1,0:T(8,128)} %get-tuple-element.352, f32[4,2,128,128]{2,3,1,0:T(8,128)S(1)} %copy.304, s32[]{:T(128)} %constant.169.clone.1..sunk, s32[]{:T(128)} %constant.169.clone.1..sunk, s32[]{:T(128)S(6)} %select_n.167, s32[]{:T(128)S(6)} %select_n.168) | dynamic-update-slice | bytes 1048580 | tf_op jit(solution)/shard_map/while/body/eval_jaxpr/dynamic_update_slice | solution.py:135
  167.1 1.1 constant_dynamic-slice_fusion.9
  168.4 1.5 constant_dynamic-slice_fusion.8
  170.3 7.7 %dynamic_update_slice.8 = f32[4,2,384,384]{2,3,1,0:T(8,128)} dynamic-update-slice(f32[4,2,384,384]{2,3,1,0:T(8,128)} %get-tuple-element.352, f32[4,2,128,128]{2,3,1,0:T(8,128)S(1)} %copy.304, s32[]{:T(128)} %constant.169.clone.1..sunk, s32[]{:T(128)} %constant.169.clone.1..sunk, s32[]{:T(128)S(6)} %select_n.167, s32[]{:T(128)S(6)} %select_n.168) | dynamic-update-slice | bytes 1048580 | tf_op jit(solution)/shard_map/while/body/eval_jaxpr/dynamic_update_slice | solution.py:135
  178.0 1.5 fusion.87
  179.5 5.2 %collective-permute-start.4 = (f32[4,2,384,64]{2,3,1,0:T(8,128)S(1)}, f32[4,2,384,64]{2,3,1,0:T(8,128)S(1)}, u32[]{:S(2)}, u32[]{:S(2)}) collective-permute-start(f32[4,2,384,64]{2,3,1,0:T(8,128)S(1)} %get-tuple-element.203), channel_id=1, source_target_pairs={{0,15},{1,0},{2,1},{3,2},{4,3},{5,4},{6,5},{7,6},{8,7},{9,8},{10,9... | collective-permute-start | bytes 2359304 | tf_op jit(solution)/shard_map/ppermute | solution.py:31
  184.7 2.1 slice.320
  186.8 29.9 %collective-permute-done.4 = f32[4,2,384,64]{2,3,1,0:T(8,128)S(1)} collective-permute-done((f32[4,2,384,64]{2,3,1,0:T(8,128)S(1)}, f32[4,2,384,64]{2,3,1,0:T(8,128)S(1)}, u32[]{:S(2)}, u32[]{:S(2)}) %collective-permute-start.4) | collective-permute-done | bytes 786464 | tf_op jit(solution)/shard_map/ppermute | solution.py:31
  216.7 1.2 add_dynamic-update-slice_fusion
  218.0 1.4 collective-permute-done.5
  219.6 1.7 fusion.88
  221.3 2.3 copy.116
  224.2 1.3 fusion.31
  225.5 0.7 pad_maximum_fusion.11
  226.3 2.3 copy.118
  228.6 3.9 collective-permute-start.7
  232.5 240.5 %all-reduce.2.cloned.1.call-done = f32[2,128,128]{1,2,0:T(8,128)} async-done(((f32[2,128,128]{1,2,0:T(8,128)}), f32[2,128,128]{1,2,0:T(8,128)}) %all-reduce.2.cloned.1.call-update) | async-done | bytes 131088 | tf_op jit(solution)/shard_map/psum | solution.py:154
  472.9 0.9 multiply_subtract_fusion.7
  473.9 0.8 copy.123
  474.6 2.0 slice.378
  476.6 2.4 copy.117
  479.0 2.3 slice_add_fusion.1
  481.3 6.5 %scatter-add.16 = f32[4,2,256,256]{2,3,1,0:T(8,128)} dynamic-update-slice(f32[4,2,256,256]{2,3,1,0:T(8,128)} %slice.378, f32[4,2,64,256]{2,3,1,0:T(8,128)} %slice_add_fusion.1, s32[]{:T(128)} %constant.169.clone.1, s32[]{:T(128)} %constant.169.clone.1, s32[]{:T(128)} %constant.180.clone.1, s32[]{:T(128)} %constant.169.clone.1) | dynamic-update-slice | bytes 1048580 | tf_op jit(solution)/shard_map/scatter-add | solution.py:148
  487.8 2.4 copy.119
  490.1 1.8 slice_add_fusion
  491.9 5.8 %scatter-add.19 = f32[4,2,256,256]{2,3,1,0:T(8,128)} dynamic-update-slice(f32[4,2,256,256]{2,3,1,0:T(8,128)} %scatter-add.16, f32[4,2,64,256]{2,3,1,0:T(8,128)S(1)} %slice_add_fusion, s32[]{:T(128)} %constant.169.clone.1, s32[]{:T(128)} %constant.169.clone.1, s32[]{:T(128)} %constant.169.clone.1, s32[]{:T(128)} %constant.169.clone.1) | dynamic-update-slice | bytes 1048580 | tf_op jit(solution)/shard_map/scatter-add | solution.py:149
  497.8 3.2 multiply_subtract_fusion
  501.0 2.9 copy.122
  (131 shorter events, 32.8 us)
Async XLA Ops:
  7.2 465.8 %all-reduce.2.cloned.1.call-start = ((), (), s32[]{:S(2)}) async-start(), calls=%async_computation | async-start | bytes 262144 | tf_op jit(solution)/shard_map/psum | solution.py:154
  9.5 9.0 %collective-permute-start = (f32[4,2,64,256]{3,2,1,0:T(8,128)}, f32[4,2,64,256]{3,2,1,0:T(8,128)}, u32[]{:S(2)}, u32[]{:S(2)}) collective-permute-start(f32[4,2,64,256]{3,2,1,0:T(8,128)} %get-tuple-element.222), channel_id=1, source_target_pairs={{0,16},{16,32},{32,48},{48,64},{64,80},{80,96},{96,112},{112,128},... | collective-permute-start | bytes 1572872 | tf_op jit(solution)/shard_map/ppermute | solution.py:20
  12.1 9.2 %collective-permute-start.1 = (f32[4,2,64,256]{3,2,1,0:T(8,128)}, f32[4,2,64,256]{3,2,1,0:T(8,128)}, u32[]{:S(2)}, u32[]{:S(2)}) collective-permute-start(f32[4,2,64,256]{3,2,1,0:T(8,128)} %get-tuple-element.223), channel_id=1, source_target_pairs={{16,0},{32,16},{48,32},{64,48},{80,64},{96,80},{112,96},{128,112},... | collective-permute-start | bytes 1572872 | tf_op jit(solution)/shard_map/ppermute | solution.py:22
  12.7 2.0 copy-start.8
  12.7 2.2 copy-start.6
  12.7 2.5 copy-start.7
  12.7 3.2 copy-start.9
  14.7 52.5 %copy-start = (f32[4,2,256,256]{2,3,1,0:T(8,128)}, f32[4,2,256,256]{2,3,1,0:T(8,128)S(1)}, u32[]{:S(2)}) copy-start(f32[4,2,256,256]{2,3,1,0:T(8,128)S(1)} %copy.120) | copy-start | bytes 6291460
  23.7 43.6 %copy-start.2 = (f32[4,2,64,256]{2,3,1,0:T(8,128)S(1)}, f32[4,2,64,256]{2,3,1,0:T(8,128)}, u32[]{:S(2)}) copy-start(f32[4,2,64,256]{2,3,1,0:T(8,128)} %copy.52) | copy-start | bytes 1572868
  23.7 43.6 %copy-start.3 = (f32[4,2,64,256]{2,3,1,0:T(8,128)S(1)}, f32[4,2,64,256]{2,3,1,0:T(8,128)}, u32[]{:S(2)}) copy-start(f32[4,2,64,256]{2,3,1,0:T(8,128)} %copy.54) | copy-start | bytes 1572868
  25.6 29.8 %collective-permute-start.2 = (f32[4,2,384,64]{2,3,1,0:T(8,128)S(1)}, f32[4,2,384,64]{2,3,1,0:T(8,128)S(1)}, u32[]{:S(2)}, u32[]{:S(2)}) collective-permute-start(f32[4,2,384,64]{2,3,1,0:T(8,128)S(1)} %get-tuple-element.204), channel_id=1, source_target_pairs={{0,1},{1,2},{2,3},{3,4},{4,5},{5,6},{6,7},{7,8},{8,9},{9,10},{10,1... | collective-permute-start | bytes 2359304 | tf_op jit(solution)/shard_map/ppermute | solution.py:20
  28.7 38.5 %collective-permute-start.3 = (f32[4,2,384,64]{2,3,1,0:T(8,128)S(1)}, f32[4,2,384,64]{2,3,1,0:T(8,128)S(1)}, u32[]{:S(2)}, u32[]{:S(2)}) collective-permute-start(f32[4,2,384,64]{2,3,1,0:T(8,128)S(1)} %get-tuple-element.205), channel_id=1, source_target_pairs={{1,0},{2,1},{3,2},{4,3},{5,4},{6,5},{7,6},{8,7},{9,8},{10,9},{11,1... | collective-permute-start | bytes 2359304 | tf_op jit(solution)/shard_map/ppermute | solution.py:22
  91.6 1.6 copy-start.4
  109.7 0.8 copy-start.5
  179.5 37.2 %collective-permute-start.4 = (f32[4,2,384,64]{2,3,1,0:T(8,128)S(1)}, f32[4,2,384,64]{2,3,1,0:T(8,128)S(1)}, u32[]{:S(2)}, u32[]{:S(2)}) collective-permute-start(f32[4,2,384,64]{2,3,1,0:T(8,128)S(1)} %get-tuple-element.203), channel_id=1, source_target_pairs={{0,15},{1,0},{2,1},{3,2},{4,3},{5,4},{6,5},{7,6},{8,7},{9,8},{10,9... | collective-permute-start | bytes 2359304 | tf_op jit(solution)/shard_map/ppermute | solution.py:31
  184.7 34.7 %collective-permute-start.5 = (f32[4,2,384,64]{2,3,1,0:T(8,128)S(1)}, f32[4,2,384,64]{2,3,1,0:T(8,128)S(1)}, u32[]{:S(2)}, u32[]{:S(2)}) collective-permute-start(f32[4,2,384,64]{2,3,1,0:T(8,128)S(1)} %get-tuple-element.202), channel_id=1, source_target_pairs={{0,1},{1,2},{2,3},{3,4},{4,5},{5,6},{6,7},{7,8},{8,9},{9,10},{10,1... | collective-permute-start | bytes 2359304 | tf_op jit(solution)/shard_map/ppermute | solution.py:31
  223.6 252.9 %collective-permute-start.6 = (f32[4,2,64,256]{3,2,1,0:T(8,128)}, f32[4,2,64,256]{3,2,1,0:T(8,128)}, u32[]{:S(2)}, u32[]{:S(2)}) collective-permute-start(f32[4,2,64,256]{3,2,1,0:T(8,128)} %copy.116), channel_id=1, source_target_pairs={{0,240},{16,0},{32,16},{48,32},{64,48},{80,64},{96,80},{112,96},{1... | collective-permute-start | bytes 1572872 | tf_op jit(solution)/shard_map/ppermute | solution.py:31
  228.6 259.2 %collective-permute-start.7 = (f32[4,2,64,256]{3,2,1,0:T(8,128)}, f32[4,2,64,256]{3,2,1,0:T(8,128)}, u32[]{:S(2)}, u32[]{:S(2)}) collective-permute-start(f32[4,2,64,256]{3,2,1,0:T(8,128)} %copy.118), channel_id=1, source_target_pairs={{0,16},{16,32},{32,48},{48,64},{64,80},{80,96},{96,112},{112,128},... | collective-permute-start | bytes 1572872 | tf_op jit(solution)/shard_map/ppermute | solution.py:31
  490.1 7.6 %copy-start.1 = (f32[4,2,256,256]{2,3,1,0:T(8,128)S(1)}, f32[4,2,256,256]{2,3,1,0:T(8,128)}, u32[]{:S(2)}) copy-start(f32[4,2,256,256]{2,3,1,0:T(8,128)} %copy-done) | copy-start | bytes 6291460
Sparse Core Ops, SparseCore 0:
  226.3 246.6 all-reduce.1
where the time goes:
time: 514 us; the launch traced here: 511 us
  waiting for transfers between devices  307 us (60%)
  local copies, waits for them, and re-layouts  112 us (22%)
  other arithmetic  21.8 us (4%)
  starting transfers between devices  21.5 us (4%)
  matrix products  17.7 us (3%)
  loops' own time  15.5 us (3%)
  between operations  14.6 us (3%)
    psum x1, waiting for transfers between devices, body(): summed = lax.psum(local_grad, ('row', 'col'))  240 us
    ppermute x4, waiting for transfers between devices, passed_along(): lax.ppermute(array, axis, [(i, (i + by) % length) for i in range(length)])  31.3 us
    dynamic_update_slice x8, local copies, waits for them, and re-layouts, deposit(): lax.dynamic_update_slice(running, lax.dynamic_slice(running, begin, piece...  31.1 us
    ppermute x2, waiting for transfers between devices, padded_2(): lax.ppermute(tail, axis, [(i, (i + 1) % count) for i in range(count)])  23.4 us
    gather x24, local copies, waits for them, and re-layouts  18.8 us
    another operation x1, loops' own time, body(): grad_pad = lax.fori_loop(0, positions, deposit, jnp.zeros_like(padded))  15.4 us
    ppermute x2, waiting for transfers between devices, padded_2(): lax.ppermute(head, axis, [((i + 1) % count, i) for i in range(count)])  12.2 us
  transfers between devices with their start and end apart: 9, of which 7 were waited for; matrix products, arithmetic and copies ran while one was open for 6% of the time, Pallas kernels for 0%

commit v1 on v0

v1 whole, which is shorter than its diff:
```python
import functools
import math

import jax
import jax.numpy as jnp
import numpy as np
from jax import lax
from jax.experimental import pallas as pl
from jax.experimental.pallas import tpu as pltpu
from jax.sharding import PartitionSpec as P

fresnel_phase = 40.0
object_step = 0.25
N = 128
T = 256
M = 64
S = 4
B = 4
F32 = jnp.float32
BF16 = jnp.bfloat16
MESH = pl.DeviceIdType.MESH


def block_pair(mat):
    re, im = mat.real, mat.imag
    right = np.block([[re, im], [-im, re]])
    left = np.block([[re, -im], [im, re]])
    out = []
    for block in (right, left):
        high = block.astype(np.float32).astype(BF16)
        low = (block - high.astype(np.float64)).astype(np.float32).astype(BF16)
        out += [high, low]
    return np.stack(out)


def tables():
    index = np.arange(N)
    dft = np.exp(-2j * np.pi * (index[:, None] * index[None, :] % N) / N) / math.sqrt(N)
    freq = ((index + N // 2) % N - N // 2) / N
    chirp = np.exp(-1j * np.pi * fresnel_phase * freq**2)
    hop = np.conj(dft) @ (chirp[:, None] * dft)
    return np.stack([block_pair(hop), block_pair(dft)])


def split(x):
    high = x.astype(BF16)
    return high, (x - high.astype(F32)).astype(BF16)


def dot(a, b):
    return jnp.dot(a, b, preferred_element_type=F32)


def both_sides(xr, xi, tab, which, conj):
    r, l = (2, 0) if conj else (0, 2)
    xh, xl = split(jnp.concatenate([xr, xi], axis=1))
    wh, wl = tab[which, r], tab[which, r + 1]
    y = dot(xh, wh) + (dot(xl, wh) + dot(xh, wl))
    cols = []
    for p in range(B):
        part = y[p * N : (p + 1) * N]
        cols.append(jnp.concatenate([part[:, :N], part[:, N:]], axis=0))
    yh, yl = split(jnp.concatenate(cols, axis=1))
    vh, vl = tab[which, l], tab[which, l + 1]
    z = dot(vh, yh) + (dot(vh, yl) + dot(vl, yh))
    zr = jnp.concatenate([z[:N, p * N : (p + 1) * N] for p in range(B)], axis=0)
    zi = jnp.concatenate([z[N:, p * N : (p + 1) * N] for p in range(B)], axis=0)
    return zr, zi


def kernel(
    n_row, n_col,
    offs, flags, obj_hbm, probe, inten, tab,
    out_obj, out_probe,
    tile, pad0, pad1, pad2, pad3, halo, sbuf, wins, psi, zbuf, gpad, rbuf, cbuf, cgot,
    pgrad, ar1, ar2, part1, part2, total,
    obj_sem, hs, hr, ps, pr, rs, rr, cs, cr, as_, ar_,
):
    pads = (pad0, pad1, pad2, pad3)
    me_r = lax.axis_index("row")
    me_c = lax.axis_index("col")
    up, down = lax.rem(me_r + n_row - 1, n_row), lax.rem(me_r + 1, n_row)
    left, right = lax.rem(me_c + n_col - 1, n_col), lax.rem(me_c + 1, n_col)
    lane = lax.broadcasted_iota(jnp.int32, (T, N), 1)
    low = lane < M

    def swap(x):
        return pltpu.roll(x, M, 1)

    def remote(src, dst, ssem, rsem, dev):
        return pltpu.make_async_remote_copy(
            src_ref=src, dst_ref=dst, send_sem=ssem, recv_sem=rsem, device_id=dev, device_id_type=MESH
        )

    loads = [pltpu.make_async_copy(obj_hbm.at[k], tile.at[k], obj_sem.at[k]) for k in range(S)]
    for c in loads:
        c.start()
    barrier = pltpu.get_barrier_semaphore()
    for d in range(1, n_row):
        pl.semaphore_signal(barrier, inc=1, device_id=(lax.rem(me_r + d, n_row), me_c), device_id_type=MESH)
    for d in range(1, n_col):
        pl.semaphore_signal(barrier, inc=1, device_id=(me_r, lax.rem(me_c + d, n_col)), device_id_type=MESH)
    pl.semaphore_wait(barrier, n_row + n_col - 2)

    sends = []
    rim = []
    for k in range(S):
        loads[k].wait()
        re, im = tile[k, 0], tile[k, 1]
        sbuf[k, 0] = jnp.where(low, re[:, :N], swap(im[:, :N]))
        sbuf[k, 1] = jnp.where(low, swap(re[:, N:]), im[:, N:])
        pair = (
            remote(sbuf.at[k, 0], halo.at[k, 1], hs.at[k, 0], hr.at[k, 1], (me_r, left)),
            remote(sbuf.at[k, 1], halo.at[k, 0], hs.at[k, 1], hr.at[k, 0], (me_r, right)),
        )
        for c in pair:
            c.start()
        sends += pair
        rim.append(pair)

    def row_rims(k, j):
        pad = pads[k]
        pair = (
            remote(pad.at[:, j, pl.ds(M, M)], pad.at[:, j, pl.ds(M + T, M)],
                   ps.at[k, j, 0], pr.at[k, j, 1], (up, me_c)),
            remote(pad.at[:, j, pl.ds(T, M)], pad.at[:, j, pl.ds(0, M)],
                   ps.at[k, j, 1], pr.at[k, j, 0], (down, me_c)),
        )
        for c in pair:
            c.start()
        sends.extend(pair)
        return pair

    rows = {k: [] for k in range(S)}
    for k in range(S):
        for ch in range(2):
            pads[k][ch, 1, M : M + T] = jnp.where(low, swap(tile[k, ch, :, :N]), swap(tile[k, ch, :, N:]))
        rows[k] += row_rims(k, 1)

    def clear(i, carry):
        zbuf[i] = jnp.zeros(zbuf.shape[1:], F32)
        return carry

    lax.fori_loop(0, zbuf.shape[0], clear, 0)

    def merge(k):
        for c in rim[k]:
            c.wait_recv()
        lo, hi = halo[k, 0], halo[k, 1]
        pads[k][0, 0, M : M + T] = jnp.where(low, lo, swap(tile[k, 0, :, :N]))
        pads[k][1, 0, M : M + T] = jnp.where(low, swap(lo), swap(tile[k, 1, :, :N]))
        pads[k][0, 2, M : M + T] = jnp.where(low, swap(tile[k, 0, :, N:]), swap(hi))
        pads[k][1, 2, M : M + T] = jnp.where(low, swap(tile[k, 1, :, N:]), hi)
        rows[k] += row_rims(k, 0)
        rows[k] += row_rims(k, 2)

    lane_n = lax.broadcasted_iota(jnp.int32, (N, N), 1)
    spots = []
    for p in range(B):
        sy, sx = offs[2 * p], offs[2 * p + 1]
        spots.append((sy, lax.shift_right_logical(sx, 7), lax.bitwise_and(sx, N - 1)))

    def windows(k):
        for c in rows[k]:
            c.wait_recv()
        for p in range(B):
            sy, q, r = spots[p]
            back = lax.bitwise_and(N - r, N - 1)
            for ch in range(2):
                a = pltpu.roll(pads[k][ch, q, pl.ds(sy, N), :], back, 1)
                b = pltpu.roll(pads[k][ch, q + 1, pl.ds(sy, N), :], back, 1)
                wins[k, ch, p * N : (p + 1) * N] = jnp.where(lane_n < N - r, a, b)

    def incident(k):
        if k == 0:
            return tuple(jnp.concatenate([probe[c]] * B, axis=0) for c in range(2))
        return psi[k - 1, 0], psi[k - 1, 1]

    def exit_wave(k):
        ar, ai = incident(k)
        wr, wi = wins[k, 0], wins[k, 1]
        return ar * wr - ai * wi, ar * wi + ai * wr

    def forward(k):
        zr, zi = both_sides(*exit_wave(k), tab, 0, False)
        psi[k, 0] = zr
        psi[k, 1] = zi

    merge(0)
    for k in range(1, S):
        merge(k)
        windows(k - 1)
        forward(k - 1)
    windows(S - 1)

    fr, fi = both_sides(*exit_wave(S - 1), tab, 1, False)
    level = jnp.concatenate([jnp.full((N, N), flags[p].astype(F32), F32) for p in range(B)], axis=0)
    excess = level * (fr * fr + fi * fi - inten[...])
    gr, gi = both_sides(excess * fr, excess * fi, tab, 1, True)

    def deposit(k, gr, gi):
        ar, ai = incident(k)
        for ch, g in enumerate((ar * gr + ai * gi, ar * gi - ai * gr)):
            for p in range(B):
                r = spots[p][2]
                g_p = pltpu.roll(g[p * N : (p + 1) * N], r, 1)
                zbuf[p * 2 + ch, 1, T : T + N] = jnp.where(lane_n >= r, g_p, 0.0)
                zbuf[p * 2 + ch, 2, T : T + N] = jnp.where(lane_n < r, g_p, 0.0)
        for ch in range(2):
            for j in range(3):
                acc = None
                for p in range(B):
                    sy, q, r = spots[p]
                    group = lax.rem(j + 1 - q + 3, 3)
                    piece = zbuf[p * 2 + ch, group, pl.ds(T - sy, T + N), :]
                    acc = piece if acc is None else acc + piece
                gpad[k, ch, j] = acc
        pair = (
            remote(gpad.at[k, :, :, pl.ds(0, M)], rbuf.at[k, 1], rs.at[k, 0], rr.at[k, 1], (up, me_c)),
            remote(gpad.at[k, :, :, pl.ds(M + T, M)], rbuf.at[k, 0], rs.at[k, 1], rr.at[k, 0], (down, me_c)),
        )
        for c in pair:
            c.start()
        sends.extend(pair)
        return pair

    def fold_rows(k, pair):
        for c in pair:
            c.wait_recv()
        gpad[k, :, :, M : 2 * M] += rbuf[k, 0]
        gpad[k, :, :, T : T + M] += rbuf[k, 1]
        body = slice(M, M + T)
        cbuf[k, 0] = jnp.where(low, gpad[k, 0, 0, body], swap(gpad[k, 1, 0, body]))
        cbuf[k, 1] = jnp.where(low, swap(gpad[k, 0, 2, body]), gpad[k, 1, 2, body])
        cols = (
            remote(cbuf.at[k, 0], cgot.at[k, 1], cs.at[k, 0], cr.at[k, 1], (me_r, left)),
            remote(cbuf.at[k, 1], cgot.at[k, 0], cs.at[k, 1], cr.at[k, 0], (me_r, right)),
        )
        for c in cols:
            c.start()
        sends.extend(cols)
        return cols

    cols = {}
    for k in range(S - 1, -1, -1):
        pair = deposit(k, gr, gi)
        wr, wi = wins[k, 0], wins[k, 1]
        gr, gi = wr * gr + wi * gi, wr * gi - wi * gr
        if k > 0:
            gr, gi = both_sides(gr, gi, tab, 0, True)
        else:
            for c, g in enumerate((gr, gi)):
                pgrad[c * N : (c + 1) * N] = (g[:N] + g[N : 2 * N]) + (g[2 * N : 3 * N] + g[3 * N :])
        cols[k] = fold_rows(k, pair)

    depth = 2 * N // n_row

    def exchange(stage, axis, pick_src, pick_dst):
        count = n_row if axis == 0 else n_col
        me = me_r if axis == 0 else me_c
        out = []
        for d in range(1, count):
            peer = lax.rem(me + d, count)
            dev = (peer, me_c) if axis == 0 else (me_r, peer)
            out.append(remote(pick_src(peer), pick_dst(me), as_.at[stage, d], ar_.at[stage, d], dev))
        for c in out:
            c.start()
        sends.extend(out)
        return out

    def rows_of(ref, i):
        return ref.at[pl.ds(pl.multiple_of(i * depth, 8), depth)]

    own = pl.ds(pl.multiple_of(me_r * depth, 8), depth)
    flow = exchange(0, 0, lambda i: rows_of(pgrad, i), lambda me: ar1.at[me])
    ar1[me_r] = pgrad[own, :]
    for c in flow:
        c.wait_recv()
    acc = ar1[0]
    for i in range(1, n_row):
        acc = acc + ar1[i]
    part1[...] = acc
    flow = exchange(1, 1, lambda i: part1, lambda me: ar2.at[me])
    ar2[me_c] = acc
    for c in flow:
        c.wait_recv()
    acc = ar2[0]
    for i in range(1, n_col):
        acc = acc + ar2[i]
    part2[...] = acc
    flow = exchange(2, 0, lambda i: part2, lambda me: rows_of(total, me))
    total[own, :] = acc
    for c in flow:
        c.wait_recv()
    factor = 1.0 / math.sqrt(B * n_row * n_col)
    for c in range(2):
        out_probe[c] = probe[c] - factor * total[c * N : (c + 1) * N]

    body = slice(M, M + T)
    for k in range(S - 1, -1, -1):
        for c in cols[k]:
            c.wait_recv()
        lo, hi = cgot[k, 0], cgot[k, 1]
        for ch in range(2):
            t0, t1, t2 = (swap(gpad[k, ch, j, body]) for j in range(3))
            lo_c, hi_c = (lo, swap(hi)) if ch == 0 else (swap(lo), hi)
            out_obj[k, ch, :, :N] = tile[k, ch, :, :N] - object_step * jnp.where(low, t0 + lo_c, t1)
            out_obj[k, ch, :, N:] = tile[k, ch, :, N:] - object_step * jnp.where(low, t1, t2 + hi_c)
    for c in sends:
        c.wait_send()


def body(n_row, n_col, object_slices, probe_wave, offsets, active_flags, intensity):
    depth = 2 * N // n_row
    vmem = pl.BlockSpec(memory_space=pltpu.VMEM)
    smem = pl.BlockSpec(memory_space=pltpu.SMEM)
    dma = pltpu.SemaphoreType.DMA
    scratch = (
        [pltpu.VMEM((S, 2, T, T), F32)]
        + [pltpu.VMEM((2, 3, T + N, N), F32)] * S
        + [
            pltpu.VMEM((S, 2, T, N), F32),
            pltpu.VMEM((S, 2, T, N), F32),
            pltpu.VMEM((S, 2, B * N, N), F32),
            pltpu.VMEM((S - 1, 2, B * N, N), F32),
            pltpu.VMEM((2 * B, 3, 2 * T + N, N), F32),
            pltpu.VMEM((S, 2, 3, T + N, N), F32),
            pltpu.VMEM((S, 2, 2, 3, M, N), F32),
            pltpu.VMEM((S, 2, T, N), F32),
            pltpu.VMEM((S, 2, T, N), F32),
            pltpu.VMEM((2 * N, N), F32),
            pltpu.VMEM((n_row, depth, N), F32),
            pltpu.VMEM((n_col, depth, N), F32),
            pltpu.VMEM((depth, N), F32),
            pltpu.VMEM((depth, N), F32),
            pltpu.VMEM((2 * N, N), F32),
        ]
        + [dma((S,)), dma((S, 2)), dma((S, 2)), dma((S, 3, 2)), dma((S, 3, 2))]
        + [dma((S, 2)), dma((S, 2)), dma((S, 2)), dma((S, 2))]
        + [dma((3, max(n_row, n_col))), dma((3, max(n_row, n_col)))]
    )
    return pl.pallas_call(
        functools.partial(kernel, n_row, n_col),
        out_shape=(
            jax.ShapeDtypeStruct((S, 2, T, T), F32),
            jax.ShapeDtypeStruct((2, N, N), F32),
        ),
        in_specs=[smem, smem, pl.BlockSpec(memory_space=pl.ANY), vmem, vmem, vmem],
        out_specs=(vmem, vmem),
        scratch_shapes=scratch,
        compiler_params=pltpu.CompilerParams(
            collective_id=0, has_side_effects=True, vmem_limit_bytes=60000000
        ),
        name="step",
    )(
        offsets.reshape(2 * B),
        active_flags.reshape(B),
        object_slices,
        probe_wave,
        intensity.reshape(B * N, N),
        jnp.asarray(tables()),
    )


def solution(mesh):
    in_specs = (
        P(None, None, "row", "col"),
        P(),
        P("row", "col", None, None),
        P("row", "col", None),
        P("row", "col", None, None, None),
    )
    out_specs = (P(None, None, "row", "col"), P())
    run = functools.partial(body, mesh.shape["row"], mesh.shape["col"])
    return jax.shard_map(run, mesh=mesh, in_specs=in_specs, out_specs=out_specs, check_vma=False)
```

time: 514 us -> 121 us (0.24)
  waiting for transfers between devices: 307 us -> 0 us
  Pallas kernels: 0 us -> 115 us
  local copies, waits for them, and re-layouts: 112 us -> 5.1 us
  other arithmetic: 21.8 us -> 0 us
  starting transfers between devices: 21.5 us -> 0 us
  matrix products: 17.7 us -> 0 us
  loops' own time: 15.5 us -> 0 us
  between operations: 14.6 us -> 0.65 us
    psum x1 -> x0, waiting for transfers between devices: 240 us -> none  [body(): summed = lax.psum(local_grad, ('row', 'col'))]
    pallas_call x0 -> x1, Pallas kernels: none -> 115 us  [body(): pl.pallas_call(functools.partial(kernel, n_row, n_col), out_shape=(jax.Sh...]
    ppermute x8 -> x0, waiting for transfers between devices: 66.9 us -> none  [the longest x4 31.3 us: passed_along(): lax.ppermute(array, axis, [(i, (i + by) % length) for i in range(length)])]
    dynamic_update_slice x8 -> x0, local copies, waits for them, and re-layouts: 31.1 us -> none  [deposit(): lax.dynamic_update_slice(running, lax.dynamic_slice(running, begin, piece...]
    ppermute x8 -> x0, starting transfers between devices: 21.5 us -> none  [the longest x4 9.62 us: passed_along(): lax.ppermute(array, axis, [(i, (i + by) % length) for i in range(length)])]
    gather x24 -> x0, local copies, waits for them, and re-layouts: 18.8 us -> none
    dot_general x28 -> x0, matrix products: 17.7 us -> none  [the longest x14 9.11 us: transform(): result = jnp.einsum('qbjk,pqkl->pbjl', left, block, precision=exact)]
    dynamic_slice x24 -> x0, local copies, waits for them, and re-layouts: 16.8 us -> none  [the longest x8 6.73 us: deposit(): lax.dynamic_slice(running, begin, piece.shape) + piece]
  transfers between devices with their start and end apart: 9 -> 0, of which waited for: 7 -> 0; matrix products, arithmetic and copies ran while one was open for 6% -> 0% of each run, Pallas kernels for 0% -> 0%
where the time goes in v1:
time: 121 us
  Pallas kernels  115 us (95%)
  local copies, waits for them, and re-layouts  5.1 us (4%)
    pallas_call x1, Pallas kernels, body(): pl.pallas_call(functools.partial(kernel, n_row, n_col), out_shape=(jax.Sh...  115 us
    unnamed x5, local copies, waits for them, and re-layouts  4.51 us

profile of v1, /device:TPU:1, one launch (start us, length us, event | category | flops | bytes accessed | tf_op | source)
XLA Modules:
  0.0 120.9 jit_solution(14381176159407898081)
XLA Ops:
  0.6 0.8 copy.9
  1.4 0.6 reshape.13.offs
  2.0 115.2 %step.1 = (f32[4,2,256,256]{3,2,1,0:T(8,128)}, f32[2,128,128]{2,1,0:T(8,128)}) custom-call(s32[8]{0:T(128)} %reshape.13.offs, s32[4]{0:T(128)} %bitcast.3, f32[4,2,256,256]{3,2,1,0:T(8,128)} %obj_hbm.1, f32[2,128,128]{2,1,0:T(8,128)} %probe.1, f32[512,128]{1,0:T(8,128)} %bitcast.2, bf16[2,4,256,256]{3,2,1,0:T(8,128)(2,1)} %constant.2.clone.tab), custom_call_target="tpu_custom_call" | custom-call | tf_op jit(solution)/shard_map/step/pallas_call | solution.py:342
  117.2 0.0 copy-start
  117.2 3.1 %copy.12 = f32[4,2,256,256]{3,2,1,0:T(8,128)} copy(f32[4,2,256,256]{3,2,1,0:T(8,128)} %get-tuple-element.4) | data formatting | bytes 4194304
  120.2 0.0 copy-done
  120.2 0.7 copy.13
Async XLA Ops:
  117.2 3.1 %copy-start = (f32[2,128,128]{2,1,0:T(8,128)S(1)}, f32[2,128,128]{2,1,0:T(8,128)}, u32[]{:S(2)}) copy-start(f32[2,128,128]{2,1,0:T(8,128)} %get-tuple-element.5) | copy-start | bytes 393220

commit v2 on v1

v2 whole, which is shorter than its diff:
```python
import functools
import math

import jax
import jax.numpy as jnp
import numpy as np
from jax import lax
from jax.experimental import pallas as pl
from jax.experimental.pallas import tpu as pltpu
from jax.sharding import PartitionSpec as P

fresnel_phase = 40.0
object_step = 0.25
N = 128
T = 256
M = 64
S = 4
B = 4
G1, YY, ZH = 8, 4, 4
VMEM_LIMIT = 52000000
F32 = jnp.float32
BF16 = jnp.bfloat16
MESH = pl.DeviceIdType.MESH


def block_pair(mat):
    re, im = mat.real, mat.imag
    right = np.block([[re, im], [-im, re]])
    left = np.block([[re, -im], [im, re]])
    out = []
    for block in (right, left):
        high = block.astype(np.float32).astype(BF16)
        low = (block - high.astype(np.float64)).astype(np.float32).astype(BF16)
        out += [high, low]
    return np.stack(out)


def tables():
    index = np.arange(N)
    dft = np.exp(-2j * np.pi * (index[:, None] * index[None, :] % N) / N) / math.sqrt(N)
    freq = ((index + N // 2) % N - N // 2) / N
    chirp = np.exp(-1j * np.pi * fresnel_phase * freq**2)
    hop = np.conj(dft) @ (chirp[:, None] * dft)
    return np.stack([block_pair(hop), block_pair(dft)])


def split(x):
    high = x.astype(BF16)
    return high, (x - high.astype(F32)).astype(BF16)


def dot(a, b):
    return jnp.dot(a, b, preferred_element_type=F32)


def both_sides(xr, xi, tab, which, conj):
    r, l = (2, 0) if conj else (0, 2)
    xh, xl = split(jnp.concatenate([xr, xi], axis=1))
    wh, wl = tab[which, r], tab[which, r + 1]
    y = dot(xh, wh) + (dot(xl, wh) + dot(xh, wl))
    cols = []
    for p in range(B):
        part = y[p * N : (p + 1) * N]
        cols.append(jnp.concatenate([part[:, :N], part[:, N:]], axis=0))
    yh, yl = split(jnp.concatenate(cols, axis=1))
    vh, vl = tab[which, l], tab[which, l + 1]
    z = dot(vh, yh) + (dot(vh, yl) + dot(vl, yh))
    zr = jnp.concatenate([z[:N, p * N : (p + 1) * N] for p in range(B)], axis=0)
    zi = jnp.concatenate([z[N:, p * N : (p + 1) * N] for p in range(B)], axis=0)
    return zr, zi


def kernel(
    n_row, n_col,
    offs, flags, obj_hbm, probe_hbm, inten_hbm, tab_hbm,
    out_obj, out_probe,
    tile, probe, inten, tab, pad0, pad1, pad2, pad3, halo, sbuf, wins, psi, zbuf, gpad, rbuf, cbuf, cgot,
    pgrad, ar1, ar2, ar3, part1, part2, part3, part4, total,
    obj_sem, in_sem, out_sem, sent, hr, pr, rr, cr, got,
):
    pads = (pad0, pad1, pad2, pad3)
    me_r = lax.axis_index("row")
    me_c = lax.axis_index("col")
    up, down = lax.rem(me_r + n_row - 1, n_row), lax.rem(me_r + 1, n_row)
    left, right = lax.rem(me_c + n_col - 1, n_col), lax.rem(me_c + 1, n_col)
    zl, j1 = lax.div(me_r, G1), lax.rem(me_r, G1)
    yy, zh = lax.div(me_c, ZH), lax.rem(me_c, ZH)
    group1 = [lax.rem(j1 + d, G1) for d in range(1, G1)]
    group2 = [lax.rem(yy + d, YY) for d in range(1, YY)]
    group3 = [(lax.rem(zl + a, 2), lax.rem(zh + b, ZH)) for a in range(2) for b in range(ZH) if a or b]
    low = lax.broadcasted_iota(jnp.int32, (T, N), 1) < M

    def low_of(x):
        return low[: x.shape[0]]

    def swap(x):
        return pltpu.roll(x, M, 1)

    def remote(src, dst, ssem, rsem, dev):
        return pltpu.make_async_remote_copy(
            src_ref=src, dst_ref=dst, send_sem=ssem, recv_sem=rsem, device_id=dev, device_id_type=MESH
        )

    loads = [pltpu.make_async_copy(obj_hbm.at[k], tile.at[k], obj_sem.at[k]) for k in range(S)]
    for c in loads:
        c.start()
    others = [
        pltpu.make_async_copy(a, b, in_sem.at[i])
        for i, (a, b) in enumerate(((probe_hbm, probe), (tab_hbm, tab), (inten_hbm, inten)))
    ]
    for c in others:
        c.start()
    barrier = pltpu.get_barrier_semaphore()
    greet = [(up, me_c), (down, me_c), (me_r, left), (me_r, right)]
    greet += [(zl * G1 + j, me_c) for j in group1]
    greet += [(me_r, y * ZH + zh) for y in group2]
    greet += [(a * G1 + j1, yy * ZH + b) for a, b in group3]
    for dev in greet:
        pl.semaphore_signal(barrier, inc=1, device_id=dev, device_id_type=MESH)

    def go(*copies):
        for c in copies:
            c.start()

    def drain(ref, sem):
        pltpu.make_async_copy(ref, ref, sem).wait()

    PARTS = (slice(0, N), slice(N, T))
    ROWS = (((slice(0, M), slice(0, M)), (slice(M, N), slice(T - M, T))), ((slice(N, T), slice(M, T - M)),))

    def pack(k):
        loads[k].wait()
        for ds, ts in ROWS[0] + ROWS[1]:
            r0, r1 = tile[k, 0, ts, :N], tile[k, 0, ts, N:]
            i0, i1 = tile[k, 1, ts, :N], tile[k, 1, ts, N:]
            m = low_of(r0)
            sbuf[k, 0, ds] = jnp.where(m, r0, swap(i0))
            sbuf[k, 1, ds] = jnp.where(m, swap(r1), i1)
            rows = slice(M + ts.start, M + ts.stop)
            pads[k][0, 2, rows] = jnp.where(m, swap(r0), swap(r1))
            pads[k][1, 2, rows] = jnp.where(m, swap(i0), swap(i1))

    def send_rim(k, part):
        rows = pl.ds(part * N, N)
        go(
            remote(sbuf.at[k, 0, rows], halo.at[k, 1, rows], sent.at[0], hr.at[k, part], (me_r, left)),
            remote(sbuf.at[k, 1, rows], halo.at[k, 0, rows], sent.at[0], hr.at[k, part], (me_r, right)),
        )

    def send_rows(k, j, n):
        pad, js = pads[k], pl.ds(j, n)
        go(
            remote(pad.at[:, js, pl.ds(M, M)], pad.at[:, js, pl.ds(M + T, M)], sent.at[1], pr.at[k], (up, me_c)),
            remote(pad.at[:, js, pl.ds(T, M)], pad.at[:, js, pl.ds(0, M)], sent.at[1], pr.at[k], (down, me_c)),
        )

    def merge(k, part):
        drain(halo.at[k, :, pl.ds(part * N, N)], hr.at[k, part])
        for ds, ts in ROWS[part]:
            lo, hi = halo[k, 0, ds], halo[k, 1, ds]
            m = low_of(lo)
            rows = slice(M + ts.start, M + ts.stop)
            pads[k][0, 0, rows] = jnp.where(m, lo, swap(tile[k, 0, ts, :N]))
            pads[k][1, 0, rows] = jnp.where(m, swap(lo), swap(tile[k, 1, ts, :N]))
            pads[k][0, 1, rows] = jnp.where(m, swap(tile[k, 0, ts, N:]), swap(hi))
            pads[k][1, 1, rows] = jnp.where(m, swap(tile[k, 1, ts, N:]), hi)
        if part == 0:
            send_rows(k, 0, 2)

    lane_n = lax.broadcasted_iota(jnp.int32, (N, N), 1)
    spots = []
    for p in range(B):
        sy, sx = offs[0, p], offs[1, p]
        spots.append((sy, lax.shift_right_logical(sx, 7), lax.bitwise_and(sx, N - 1)))

    def windows(k):
        drain(rbuf.at[k], pr.at[k])
        for p in range(B):
            sy, q, r = spots[p]
            back = lax.bitwise_and(N - r, N - 1)
            for ch in range(2):
                a = pltpu.roll(pads[k][ch, 2 * q, pl.ds(sy, N), :], back, 1)
                b = pltpu.roll(pads[k][ch, 2 - q, pl.ds(sy, N), :], back, 1)
                wins[k, ch, p * N : (p + 1) * N] = jnp.where(lane_n < N - r, a, b)

    def incident(k):
        if k == 0:
            return tuple(jnp.concatenate([probe[c]] * B, axis=0) for c in range(2))
        return psi[k - 1, 0], psi[k - 1, 1]

    def exit_wave(k):
        ar, ai = incident(k)
        wr, wi = wins[k, 0], wins[k, 1]
        return ar * wr - ai * wi, ar * wi + ai * wr

    def forward(k):
        zr, zi = both_sides(*exit_wave(k), tab, 0, False)
        psi[k, 0] = zr
        psi[k, 1] = zi

    pack(0)
    pl.semaphore_wait(barrier, len(greet))
    send_rim(0, 0)
    send_rows(0, 2, 1)
    pack(1)
    send_rim(1, 0)
    send_rim(0, 1)
    send_rows(1, 2, 1)
    pack(2)
    pack(3)

    def clear(i, carry):
        zbuf[i] = jnp.zeros(zbuf.shape[1:], F32)
        return carry

    lax.fori_loop(0, zbuf.shape[0], clear, 0)
    for c in others:
        c.wait()

    merge(0, 0)
    send_rim(2, 0)
    send_rim(1, 1)
    send_rows(2, 2, 1)
    merge(1, 0)
    send_rim(3, 0)
    send_rim(2, 1)
    send_rows(3, 2, 1)
    merge(0, 1)
    windows(0)
    forward(0)
    merge(2, 0)
    send_rim(3, 1)
    merge(1, 1)
    windows(1)
    forward(1)
    merge(3, 0)
    merge(2, 1)
    windows(2)
    forward(2)
    merge(3, 1)
    windows(3)

    fr, fi = both_sides(*exit_wave(S - 1), tab, 1, False)
    level = jnp.concatenate([jnp.full((N, N), flags[p].astype(F32), F32) for p in range(B)], axis=0)
    excess = level * (fr * fr + fi * fi - inten[...])
    gr, gi = both_sides(excess * fr, excess * fi, tab, 1, True)

    def pack_cols(k, part):
        for ds, ts in ROWS[part]:
            rows = slice(M + ts.start, M + ts.stop)
            m = low_of(gpad[k, 0, 0, rows])
            cbuf[k, 0, ds] = jnp.where(m, gpad[k, 0, 0, rows], swap(gpad[k, 1, 0, rows]))
            cbuf[k, 1, ds] = jnp.where(m, swap(gpad[k, 0, 2, rows]), gpad[k, 1, 2, rows])
        rows = pl.ds(part * N, N)
        go(
            remote(cbuf.at[k, 0, rows], cgot.at[k, 1, rows], sent.at[2], cr.at[k, part], (me_r, left)),
            remote(cbuf.at[k, 1, rows], cgot.at[k, 0, rows], sent.at[2], cr.at[k, part], (me_r, right)),
        )

    def deposit(k, gr, gi):
        ar, ai = incident(k)
        for ch, g in enumerate((ar * gr + ai * gi, ar * gi - ai * gr)):
            for p in range(B):
                r = spots[p][2]
                g_p = pltpu.roll(g[p * N : (p + 1) * N], r, 1)
                zbuf[p * 2 + ch, 1, T : T + N] = jnp.where(lane_n >= r, g_p, 0.0)
                zbuf[p * 2 + ch, 2, T : T + N] = jnp.where(lane_n < r, g_p, 0.0)
        for ch in range(2):
            for j in range(3):
                acc = None
                for p in range(B):
                    sy, q, r = spots[p]
                    group = lax.rem(j + 1 - q + 3, 3)
                    piece = zbuf[p * 2 + ch, group, pl.ds(T - sy, T + N), :]
                    acc = piece if acc is None else acc + piece
                gpad[k, ch, j] = acc
        go(
            remote(gpad.at[k, :, :, pl.ds(0, M)], rbuf.at[k, 1], sent.at[3], rr.at[k], (up, me_c)),
            remote(gpad.at[k, :, :, pl.ds(M + T, M)], rbuf.at[k, 0], sent.at[3], rr.at[k], (down, me_c)),
        )
        pack_cols(k, 1)

    def fold_rows(k):
        drain(rbuf.at[k], rr.at[k])
        gpad[k, :, :, M : 2 * M] += rbuf[k, 0]
        gpad[k, :, :, T : T + M] += rbuf[k, 1]
        pack_cols(k, 0)

    for k in range(S - 1, -1, -1):
        deposit(k, gr, gi)
        wr, wi = wins[k, 0], wins[k, 1]
        gr, gi = wr * gr + wi * gi, wr * gi - wi * gr
        if k > 0:
            gr, gi = both_sides(gr, gi, tab, 0, True)
    for c, g in enumerate((gr, gi)):
        pgrad[c * N : (c + 1) * N] = (g[:N] + g[N : 2 * N]) + (g[2 * N : 3 * N] + g[3 * N :])

    D1 = 2 * N // G1
    D2 = D1 // YY

    def at(ref, i, depth):
        return ref.at[pl.ds(pl.multiple_of(i * depth, 8), depth)]

    def sum_of(ref):
        acc = ref[0]
        for i in range(1, ref.shape[0]):
            acc = acc + ref[i]
        return acc

    def arrive(stage, ref):
        drain(ref.at[pl.ds(0, ref.shape[0] - ref.shape[0] // COUNT[stage])], got.at[stage])

    COUNT = (G1, YY, 2 * ZH, YY, G1)
    go(*[
        remote(at(pgrad, j, D1), ar1.at[j1], sent.at[4], got.at[0], (zl * G1 + j, me_c))
        for j in group1
    ])
    ar1[j1] = pgrad[pl.ds(pl.multiple_of(j1 * D1, 8), D1), :]
    arrive(0, ar1)
    part1[...] = sum_of(ar1)
    go(*[
        remote(at(part1, y, D2), ar2.at[yy], sent.at[5], got.at[1], (me_r, y * ZH + zh))
        for y in group2
    ])
    ar2[yy] = part1[pl.ds(pl.multiple_of(yy * D2, 8), D2), :]
    arrive(1, ar2)
    zz = zh * 2 + zl
    acc = sum_of(ar2)
    part2[...] = acc
    ar3[zz] = acc
    go(*[
        remote(part2, ar3.at[zz], sent.at[6], got.at[2], (a * G1 + j1, yy * ZH + b))
        for a, b in group3
    ])
    fold_rows(3)
    fold_rows(2)
    fold_rows(1)
    fold_rows(0)

    def finish(k):
        for part in range(2):
            drain(cgot.at[k, :, pl.ds(part * N, N)], cr.at[k, part])
            for ds, ts in ROWS[part]:
                lo, hi = cgot[k, 0, ds], cgot[k, 1, ds]
                rows = slice(M + ts.start, M + ts.stop)
                m = low_of(lo)
                for ch in range(2):
                    t0, t1, t2 = (swap(gpad[k, ch, j, rows]) for j in range(3))
                    lo_c, hi_c = (lo, swap(hi)) if ch == 0 else (swap(lo), hi)
                    tile[k, ch, ts, :N] -= object_step * jnp.where(m, t0 + lo_c, t1)
                    tile[k, ch, ts, N:] -= object_step * jnp.where(m, t1, t2 + hi_c)
        c = pltpu.make_async_copy(tile.at[k], out_obj.at[k], out_sem.at[k])
        c.start()
        return c

    arrive(2, ar3)
    acc = sum_of(ar3)
    part3[...] = acc
    part4[pl.ds(pl.multiple_of(yy * D2, 8), D2), :] = acc
    go(*[
        remote(part3, at(part4, yy, D2), sent.at[7], got.at[3], (me_r, y * ZH + zh))
        for y in group2
    ])
    arrive(3, part4)
    go(*[
        remote(part4, at(total, j1, D1), sent.at[8], got.at[4], (zl * G1 + j, me_c))
        for j in group1
    ])
    total[pl.ds(pl.multiple_of(j1 * D1, 8), D1), :] = part4[...]
    stores = [finish(3), finish(2)]
    arrive(4, total)
    factor = 1.0 / math.sqrt(B * n_row * n_col)
    for c in range(2):
        out_probe[c] = probe[c] - factor * total[c * N : (c + 1) * N]
    stores += [finish(1), finish(0)]
    drain(sbuf, sent.at[0])
    drain(rbuf, sent.at[1])
    drain(cbuf, sent.at[2])
    drain(rbuf, sent.at[3])
    for stage, ref in enumerate((ar1, ar2, ar3, part4, total)):
        drain(ref.at[pl.ds(0, ref.shape[0] - ref.shape[0] // COUNT[stage])], sent.at[4 + stage])
    for c in stores:
        c.wait()


def body(n_row, n_col, object_slices, probe_wave, offsets, active_flags, intensity):
    vmem = pl.BlockSpec(memory_space=pltpu.VMEM)
    smem = pl.BlockSpec(memory_space=pltpu.SMEM)
    hbm = pl.BlockSpec(memory_space=pltpu.HBM)
    dma = pltpu.SemaphoreType.DMA

    def stay(x):
        return pltpu.with_memory_space_constraint(x, pltpu.HBM)

    scratch = (
        [
            pltpu.VMEM((S, 2, T, T), F32),
            pltpu.VMEM((2, N, N), F32),
            pltpu.VMEM((B * N, N), F32),
            pltpu.VMEM((2, 4, 2 * N, 2 * N), BF16),
        ]
        + [pltpu.VMEM((2, 3, T + N, N), F32)] * S
        + [
            pltpu.VMEM((S, 2, T, N), F32),
            pltpu.VMEM((S, 2, T, N), F32),
            pltpu.VMEM((S, 2, B * N, N), F32),
            pltpu.VMEM((S - 1, 2, B * N, N), F32),
            pltpu.VMEM((2 * B, 3, 2 * T + N, N), F32),
            pltpu.VMEM((S, 2, 3, T + N, N), F32),
            pltpu.VMEM((S, 2, 2, 3, M, N), F32),
            pltpu.VMEM((S, 2, T, N), F32),
            pltpu.VMEM((S, 2, T, N), F32),
            pltpu.VMEM((2 * N, N), F32),
            pltpu.VMEM((G1, 2 * N // G1, N), F32),
            pltpu.VMEM((YY, 8, N), F32),
            pltpu.VMEM((2 * ZH, 8, N), F32),
            pltpu.VMEM((2 * N // G1, N), F32),
            pltpu.VMEM((8, N), F32),
            pltpu.VMEM((8, N), F32),
            pltpu.VMEM((2 * N // G1, N), F32),
            pltpu.VMEM((2 * N, N), F32),
        ]
        + [dma((S,)), dma((3,)), dma((S,)), dma((9,))]
        + [dma((S, 2)), dma((S,)), dma((S,)), dma((S, 2)), dma((5,))]
    )
    return pl.pallas_call(
        functools.partial(kernel, n_row, n_col),
        out_shape=(
            jax.ShapeDtypeStruct((S, 2, T, T), F32),
            jax.ShapeDtypeStruct((2, N, N), F32),
        ),
        in_specs=[smem, smem, hbm, hbm, hbm, hbm],
        out_specs=(pl.BlockSpec(memory_space=pl.ANY), vmem),
        scratch_shapes=scratch,
        compiler_params=pltpu.CompilerParams(
            collective_id=0, has_side_effects=True, vmem_limit_bytes=VMEM_LIMIT
        ),
        name="step",
    )(
        stay(jnp.transpose(offsets.reshape(B, 2))),
        stay(active_flags.reshape(B)),
        stay(object_slices),
        stay(probe_wave),
        stay(intensity.reshape(B * N, N)),
        stay(jnp.asarray(tables())),
    )


def solution(mesh):
    in_specs = (
        P(None, None, "row", "col"),
        P(),
        P("row", "col", None, None),
        P("row", "col", None),
        P("row", "col", None, None, None),
    )
    out_specs = (P(None, None, "row", "col"), P())
    run = functools.partial(body, mesh.shape["row"], mesh.shape["col"])
    return jax.shard_map(run, mesh=mesh, in_specs=in_specs, out_specs=out_specs, check_vma=False)
```

time: 121 us -> 86.2 us (0.71)
  Pallas kernels: 115 us -> 82.9 us
  local copies, waits for them, and re-layouts: 5.1 us -> 1.98 us
    pallas_call x1, Pallas kernels: 115 us -> 82.9 us  [body(): pl.pallas_call(functools.partial(kernel, n_row, n_col), out_shape=(jax.Sh...]
    unnamed x5 -> x2, local copies, waits for them, and re-layouts: 4.51 us -> 1.98 us
where the time goes in v2:
time: 86.2 us; the launch traced here: 85.5 us
  Pallas kernels  82.9 us (96%)
  local copies, waits for them, and re-layouts  1.98 us (2%)
    pallas_call x1, Pallas kernels, body(): pl.pallas_call(functools.partial(kernel, n_row, n_col), out_shape=(jax.Sh...  82.9 us
    unnamed x2, local copies, waits for them, and re-layouts  1.98 us

profile of v2, /device:TPU:1, one launch (start us, length us, event | category | flops | bytes accessed | tf_op | source)
XLA Modules:
  0.0 85.5 jit_solution(12197556444803597675)
XLA Ops:
  0.6 82.9 %step.1 = (f32[4,2,256,256]{3,2,1,0:T(8,128)S(1)}, f32[2,128,128]{2,1,0:T(8,128)S(1)}) custom-call(s32[2,4]{1,0:T(2,128)} %bitcast.6, s32[4]{0:T(128)} %bitcast.7, f32[4,2,256,256]{3,2,1,0:T(8,128)} %obj_hbm.1, f32[2,128,128]{2,1,0:T(8,128)} %probe_hbm.1, f32[512,128]{1,0:T(8,128)} %bitcast.5, bf16[2,4,256,256]{3,2,1,0:T(8,128)(2,1)} %constant.2.clone.tab_hbm), custom_call_target="tpu_custom_call" | custom-call | tf_op jit(solution)/shard_map/step/pallas_call | solution.py:426
  83.5 1.3 %copy.10 = f32[4,2,256,256]{3,2,1,0:T(8,128)} copy(f32[4,2,256,256]{3,2,1,0:T(8,128)S(1)} %get-tuple-element.4) | data formatting | bytes 4194304
  84.8 0.7 copy.11

commit v3 on v2

--- a/solution.py
+++ b/solution.py
@@ -17,6 +17,7 @@
 S = 4
 B = 4
 G1, YY, ZH = 8, 4, 4
+RELAY_NEAR = True
 VMEM_LIMIT = 52000000
 F32 = jnp.float32
 BF16 = jnp.bfloat16
@@ -75,8 +76,8 @@
     offs, flags, obj_hbm, probe_hbm, inten_hbm, tab_hbm,
     out_obj, out_probe,
     tile, probe, inten, tab, pad0, pad1, pad2, pad3, halo, sbuf, wins, psi, zbuf, gpad, rbuf, cbuf, cgot,
-    pgrad, ar1, ar2, ar3, part1, part2, part3, part4, total,
-    obj_sem, in_sem, out_sem, sent, hr, pr, rr, cr, got,
+    pgrad, ar1, ar2, ar3, part1, part2, part3, part4, total, relay,
+    obj_sem, in_sem, out_sem, sent, hr, pr, rr, cr, got, relay_got, relay_sent,
 ):
     pads = (pad0, pad1, pad2, pad3)
     me_r = lax.axis_index("row")
@@ -89,6 +90,10 @@
     group2 = [lax.rem(yy + d, YY) for d in range(1, YY)]
     group3 = [(lax.rem(zl + a, 2), lax.rem(zh + b, ZH)) for a in range(2) for b in range(ZH) if a or b]
     low = lax.broadcasted_iota(jnp.int32, (T, N), 1) < M
+    zo = 1 - zl
+    z_relay, z_final = (zl, zo) if RELAY_NEAR else (zo, zl)
+    relay_up, relay_down = z_relay * G1 + 2, z_relay * G1 + G1 - 3
+    final_up, final_down = z_final * G1 + G1 - 1, z_final * G1
 
     def low_of(x):
         return low[: x.shape[0]]
@@ -115,6 +120,8 @@
     greet += [(zl * G1 + j, me_c) for j in group1]
     greet += [(me_r, y * ZH + zh) for y in group2]
     greet += [(a * G1 + j1, yy * ZH + b) for a, b in group3]
+    reach = 3 if RELAY_NEAR else 2
+    greet += [(zo * G1 + lax.rem(j1 + d, G1), me_c) for d in (reach, G1 - reach)]
     for dev in greet:
         pl.semaphore_signal(barrier, inc=1, device_id=dev, device_id_type=MESH)
 
@@ -147,12 +154,54 @@
             remote(sbuf.at[k, 1, rows], halo.at[k, 0, rows], sent.at[0], hr.at[k, part], (me_r, right)),
         )
 
-    def send_rows(k, j, n):
-        pad, js = pads[k], pl.ds(j, n)
+    def send_rows(src, top, bottom, ssem, rsem):
+        side = pl.ds(0, 2)
         go(
-            remote(pad.at[:, js, pl.ds(M, M)], pad.at[:, js, pl.ds(M + T, M)], sent.at[1], pr.at[k], (up, me_c)),
-            remote(pad.at[:, js, pl.ds(T, M)], pad.at[:, js, pl.ds(0, M)], sent.at[1], pr.at[k], (down, me_c)),
+            remote(src.at[:, side, top[0]], top[1].at[:, side], ssem, rsem, (up, me_c)),
+            remote(src.at[:, side, bottom[0]], bottom[1].at[:, side], ssem, rsem, (down, me_c)),
         )
+
+    def send_middle(src, top, bottom, ssem, rsem, slot):
+        for (rows, dst), edge, dev, hop in (
+            (top, j1 == 0, up, relay_up), (bottom, j1 == G1 - 1, down, relay_down)
+        ):
+            @pl.when(edge)
+            def _():
+                remote(src.at[:, 2, rows], relay.at[slot], ssem, relay_got.at[slot], (hop, me_c)).start()
+
+            @pl.when(jnp.logical_not(edge))
+            def _():
+                remote(src.at[:, 2, rows], dst.at[:, 2], ssem, rsem, (dev, me_c)).start()
+
+    def pass_on(top, bottom, rsem, slot):
+        for dst, here, dev in ((top, j1 == 2, final_up), (bottom, j1 == G1 - 3, final_down)):
+            @pl.when(here)
+            def _():
+                drain(relay.at[slot], relay_got.at[slot])
+                remote(relay.at[slot], dst.at[:, 2], relay_sent, rsem, (dev, me_c)).start()
+
+    def in_top(k):
+        return pads[k].at[:, :, pl.ds(M + T, M)]
+
+    def in_bottom(k):
+        return pads[k].at[:, :, pl.ds(0, M)]
+
+    def in_args(k):
+        return pads[k], (pl.ds(M, M), in_top(k)), (pl.ds(T, M), in_bottom(k)), sent.at[1], pr.at[k]
+
+    def middle_in(k):
+        send_middle(*in_args(k), k)
+
+    def relay_in(k):
+        pass_on(in_top(k), in_bottom(k), pr.at[k], k)
+
+    def out_args(k):
+        return (
+            gpad.at[k], (pl.ds(0, M), rbuf.at[k, 1]), (pl.ds(M + T, M), rbuf.at[k, 0]), sent.at[3], rr.at[k]
+        )
+
+    def relay_out(k):
+        pass_on(rbuf.at[k, 1], rbuf.at[k, 0], rr.at[k], S + k)
 
     def merge(k, part):
         drain(halo.at[k, :, pl.ds(part * N, N)], hr.at[k, part])
@@ -165,7 +214,7 @@
             pads[k][0, 1, rows] = jnp.where(m, swap(tile[k, 0, ts, N:]), swap(hi))
             pads[k][1, 1, rows] = jnp.where(m, swap(tile[k, 1, ts, N:]), hi)
         if part == 0:
-            send_rows(k, 0, 2)
+            send_rows(*in_args(k))
 
     lane_n = lax.broadcasted_iota(jnp.int32, (N, N), 1)
     spots = []
@@ -201,13 +250,14 @@
     pack(0)
     pl.semaphore_wait(barrier, len(greet))
     send_rim(0, 0)
-    send_rows(0, 2, 1)
+    middle_in(0)
     pack(1)
     send_rim(1, 0)
-    send_rim(0, 1)
-    send_rows(1, 2, 1)
+    middle_in(1)
     pack(2)
+    middle_in(2)
     pack(3)
+    middle_in(3)
 
     def clear(i, carry):
         zbuf[i] = jnp.zeros(zbuf.shape[1:], F32)
@@ -218,22 +268,25 @@
         c.wait()
 
     merge(0, 0)
+    send_rim(0, 1)
     send_rim(2, 0)
+    relay_in(0)
+    relay_in(1)
+    merge(1, 0)
     send_rim(1, 1)
-    send_rows(2, 2, 1)
-    merge(1, 0)
     send_rim(3, 0)
+    relay_in(2)
+    relay_in(3)
+    merge(0, 1)
+    merge(2, 0)
     send_rim(2, 1)
-    send_rows(3, 2, 1)
-    merge(0, 1)
     windows(0)
     forward(0)
-    merge(2, 0)
+    merge(1, 1)
+    merge(3, 0)
     send_rim(3, 1)
-    merge(1, 1)
     windows(1)
     forward(1)
-    merge(3, 0)
     merge(2, 1)
     windows(2)
     forward(2)
@@ -250,7 +303,7 @@
             rows = slice(M + ts.start, M + ts.stop)
             m = low_of(gpad[k, 0, 0, rows])
             cbuf[k, 0, ds] = jnp.where(m, gpad[k, 0, 0, rows], swap(gpad[k, 1, 0, rows]))
-            cbuf[k, 1, ds] = jnp.where(m, swap(gpad[k, 0, 2, rows]), gpad[k, 1, 2, rows])
+            cbuf[k, 1, ds] = jnp.where(m, swap(gpad[k, 0, 1, rows]), gpad[k, 1, 1, rows])
         rows = pl.ds(part * N, N)
         go(
             remote(cbuf.at[k, 0, rows], cgot.at[k, 1, rows], sent.at[2], cr.at[k, part], (me_r, left)),
@@ -273,11 +326,9 @@
                     group = lax.rem(j + 1 - q + 3, 3)
                     piece = zbuf[p * 2 + ch, group, pl.ds(T - sy, T + N), :]
                     acc = piece if acc is None else acc + piece
-                gpad[k, ch, j] = acc
-        go(
-            remote(gpad.at[k, :, :, pl.ds(0, M)], rbuf.at[k, 1], sent.at[3], rr.at[k], (up, me_c)),
-            remote(gpad.at[k, :, :, pl.ds(M + T, M)], rbuf.at[k, 0], sent.at[3], rr.at[k], (down, me_c)),
-        )
+                gpad[k, ch, (0, 2, 1)[j]] = acc
+        send_rows(*out_args(k))
+        send_middle(*out_args(k), S + k)
         pack_cols(k, 1)
 
     def fold_rows(k):
@@ -316,6 +367,8 @@
         for j in group1
     ])
     ar1[j1] = pgrad[pl.ds(pl.multiple_of(j1 * D1, 8), D1), :]
+    for k in range(S - 1, -1, -1):
+        relay_out(k)
     arrive(0, ar1)
     part1[...] = sum_of(ar1)
     go(*[
@@ -345,7 +398,7 @@
                 rows = slice(M + ts.start, M + ts.stop)
                 m = low_of(lo)
                 for ch in range(2):
-                    t0, t1, t2 = (swap(gpad[k, ch, j, rows]) for j in range(3))
+                    t0, t1, t2 = (swap(gpad[k, ch, j, rows]) for j in (0, 2, 1))
                     lo_c, hi_c = (lo, swap(hi)) if ch == 0 else (swap(lo), hi)
                     tile[k, ch, ts, :N] -= object_step * jnp.where(m, t0 + lo_c, t1)
                     tile[k, ch, ts, N:] -= object_step * jnp.where(m, t1, t2 + hi_c)
@@ -374,6 +427,11 @@
         out_probe[c] = probe[c] - factor * total[c * N : (c + 1) * N]
     stores += [finish(1), finish(0)]
     drain(sbuf, sent.at[0])
+
+    @pl.when(jnp.logical_or(j1 == 2, j1 == G1 - 3))
+    def _():
+        drain(relay, relay_sent)
+
     drain(rbuf, sent.at[1])
     drain(cbuf, sent.at[2])
     drain(rbuf, sent.at[3])
@@ -419,9 +477,10 @@
             pltpu.VMEM((8, N), F32),
             pltpu.VMEM((2 * N // G1, N), F32),
             pltpu.VMEM((2 * N, N), F32),
+            pltpu.VMEM((2 * S, 2, M, N), F32),
         ]
         + [dma((S,)), dma((3,)), dma((S,)), dma((9,))]
-        + [dma((S, 2)), dma((S,)), dma((S,)), dma((S, 2)), dma((5,))]
+        + [dma((S, 2)), dma((S,)), dma((S,)), dma((S, 2)), dma((5,)), dma((2 * S,)), dma]
     )
     return pl.pallas_call(
         functools.partial(kernel, n_row, n_col),

time: 86.2 us -> 81.4 us (0.944)
  Pallas kernels: 82.9 us -> 78.3 us
    pallas_call x1, Pallas kernels: 82.9 us -> 78.3 us  [body(): pl.pallas_call(functools.partial(kernel, n_row, n_col), out_shape=(jax.Sh...]
where the time goes in v3:
time: 81.4 us; the launch traced here: 80.9 us
  Pallas kernels  78.3 us (96%)
  local copies, waits for them, and re-layouts  1.98 us (2%)
    pallas_call x1, Pallas kernels, body(): pl.pallas_call(functools.partial(kernel, n_row, n_col), out_shape=(jax.Sh...  78.3 us
    unnamed x2, local copies, waits for them, and re-layouts  1.98 us

profile of v3, /device:TPU:1, one launch (start us, length us, event | category | flops | bytes accessed | tf_op | source)
XLA Modules:
  0.0 80.9 jit_solution(16259423168300837149)
XLA Ops:
  0.6 78.3 %step.1 = (f32[4,2,256,256]{3,2,1,0:T(8,128)S(1)}, f32[2,128,128]{2,1,0:T(8,128)S(1)}) custom-call(s32[2,4]{1,0:T(2,128)} %bitcast.6, s32[4]{0:T(128)} %bitcast.7, f32[4,2,256,256]{3,2,1,0:T(8,128)} %obj_hbm.1, f32[2,128,128]{2,1,0:T(8,128)} %probe_hbm.1, f32[512,128]{1,0:T(8,128)} %bitcast.5, bf16[2,4,256,256]{3,2,1,0:T(8,128)(2,1)} %constant.2.clone.tab_hbm), custom_call_target="tpu_custom_call" | custom-call | tf_op jit(solution)/shard_map/step/pallas_call | solution.py:485
  79.0 1.3 %copy.10 = f32[4,2,256,256]{3,2,1,0:T(8,128)} copy(f32[4,2,256,256]{3,2,1,0:T(8,128)S(1)} %get-tuple-element.4) | data formatting | bytes 4194304
  80.3 0.7 copy.11

commit v4 on v3

--- a/solution.py
+++ b/solution.py
@@ -73,10 +73,10 @@
 
 def kernel(
     n_row, n_col,
-    offs, flags, obj_hbm, probe_hbm, inten_hbm, tab_hbm,
+    offs_hbm, flags_hbm, obj_hbm, probe_hbm, inten_hbm, tab_hbm,
     out_obj, out_probe,
     tile, probe, inten, tab, pad0, pad1, pad2, pad3, halo, sbuf, wins, psi, zbuf, gpad, rbuf, cbuf, cgot,
-    pgrad, ar1, ar2, ar3, part1, part2, part3, part4, total, relay,
+    pgrad, ar1, ar2, ar3, part1, part2, part3, part4, total, relay, offs, flags,
     obj_sem, in_sem, out_sem, sent, hr, pr, rr, cr, got, relay_got, relay_sent,
 ):
     pads = (pad0, pad1, pad2, pad3)
@@ -111,7 +111,9 @@
         c.start()
     others = [
         pltpu.make_async_copy(a, b, in_sem.at[i])
-        for i, (a, b) in enumerate(((probe_hbm, probe), (tab_hbm, tab), (inten_hbm, inten)))
+        for i, (a, b) in enumerate(
+            ((offs_hbm, offs), (flags_hbm, flags), (probe_hbm, probe), (tab_hbm, tab), (inten_hbm, inten))
+        )
     ]
     for c in others:
         c.start()
@@ -218,9 +220,6 @@
 
     lane_n = lax.broadcasted_iota(jnp.int32, (N, N), 1)
     spots = []
-    for p in range(B):
-        sy, sx = offs[0, p], offs[1, p]
-        spots.append((sy, lax.shift_right_logical(sx, 7), lax.bitwise_and(sx, N - 1)))
 
     def windows(k):
         drain(rbuf.at[k], pr.at[k])
@@ -266,6 +265,9 @@
     lax.fori_loop(0, zbuf.shape[0], clear, 0)
     for c in others:
         c.wait()
+    for p in range(B):
+        sy, sx = offs[0, p], offs[1, p]
+        spots.append((sy, lax.shift_right_logical(sx, 7), lax.bitwise_and(sx, N - 1)))
 
     merge(0, 0)
     send_rim(0, 1)
@@ -478,8 +480,10 @@
             pltpu.VMEM((2 * N // G1, N), F32),
             pltpu.VMEM((2 * N, N), F32),
             pltpu.VMEM((2 * S, 2, M, N), F32),
+            pltpu.SMEM((2, B), jnp.int32),
+            pltpu.SMEM((B,), jnp.int32),
         ]
-        + [dma((S,)), dma((3,)), dma((S,)), dma((9,))]
+        + [dma((S,)), dma((5,)), dma((S,)), dma((9,))]
         + [dma((S, 2)), dma((S,)), dma((S,)), dma((S, 2)), dma((5,)), dma((2 * S,)), dma]
     )
     return pl.pallas_call(
@@ -488,7 +492,7 @@
             jax.ShapeDtypeStruct((S, 2, T, T), F32),
             jax.ShapeDtypeStruct((2, N, N), F32),
         ),
-        in_specs=[smem, smem, hbm, hbm, hbm, hbm],
+        in_specs=[hbm, hbm, hbm, hbm, hbm, hbm],
         out_specs=(pl.BlockSpec(memory_space=pl.ANY), vmem),
         scratch_shapes=scratch,
         compiler_params=pltpu.CompilerParams(

time: 81.4 us -> 80.1 us (0.984)
  Pallas kernels: 78.3 us -> 77.3 us
    pallas_call x1, Pallas kernels: 78.3 us -> 77.3 us  [body(): pl.pallas_call(functools.partial(kernel, n_row, n_col), out_shape=(jax.Sh...]
where the time goes in v4:
time: 80.1 us; the launch traced here: 80 us
  Pallas kernels  77.3 us (97%)
  local copies, waits for them, and re-layouts  1.98 us (2%)
    pallas_call x1, Pallas kernels, body(): pl.pallas_call(functools.partial(kernel, n_row, n_col), out_shape=(jax.Sh...  77.3 us
    unnamed x2, local copies, waits for them, and re-layouts  1.98 us

profile of v4, /device:TPU:1, one launch (start us, length us, event | category | flops | bytes accessed | tf_op | source)
XLA Modules:
  0.0 80.0 jit_solution(15590757152306773051)
XLA Ops:
  0.6 77.3 %step.1 = (f32[4,2,256,256]{3,2,1,0:T(8,128)S(1)}, f32[2,128,128]{2,1,0:T(8,128)S(1)}) custom-call(s32[2,4]{1,0:T(2,128)} %bitcast.6, s32[4]{0:T(128)} %bitcast.7, f32[4,2,256,256]{3,2,1,0:T(8,128)} %obj_hbm.1, f32[2,128,128]{2,1,0:T(8,128)} %probe_hbm.1, f32[512,128]{1,0:T(8,128)} %bitcast.5, bf16[2,4,256,256]{3,2,1,0:T(8,128)(2,1)} %constant.2.clone.tab_hbm), custom_call_target="tpu_custom_call" | custom-call | tf_op jit(solution)/shard_map/step/pallas_call | solution.py:489
  78.0 1.3 %copy.10 = f32[4,2,256,256]{3,2,1,0:T(8,128)} copy(f32[4,2,256,256]{3,2,1,0:T(8,128)S(1)} %get-tuple-element.4) | data formatting | bytes 4194304
  79.3 0.7 copy.11

commit v5 on v4

--- a/solution.py
+++ b/solution.py
@@ -393,7 +393,7 @@
     fold_rows(0)
 
     def finish(k):
-        for part in range(2):
+        for part in (1, 0):
             drain(cgot.at[k, :, pl.ds(part * N, N)], cr.at[k, part])
             for ds, ts in ROWS[part]:
                 lo, hi = cgot[k, 0, ds], cgot[k, 1, ds]

time: 80.1 us -> 81.9 us (1.022)
  the two profiles are of different devices: /device:TPU:1 before, /device:TPU:17 now
where the time goes in v5:
time: 81.9 us; the launch traced here: 81.8 us
  Pallas kernels  79.1 us (97%)
  local copies, waits for them, and re-layouts  1.98 us (2%)
    pallas_call x1, Pallas kernels, body(): pl.pallas_call(functools.partial(kernel, n_row, n_col), out_shape=(jax.Sh...  79.1 us
    unnamed x2, local copies, waits for them, and re-layouts  1.98 us

profile of v5, /device:TPU:17, one launch (start us, length us, event | category | flops | bytes accessed | tf_op | source)
XLA Modules:
  0.0 81.8 jit_solution(13320680665087034856)
XLA Ops:
  0.6 79.1 %step.1 = (f32[4,2,256,256]{3,2,1,0:T(8,128)S(1)}, f32[2,128,128]{2,1,0:T(8,128)S(1)}) custom-call(s32[2,4]{1,0:T(2,128)} %bitcast.6, s32[4]{0:T(128)} %bitcast.7, f32[4,2,256,256]{3,2,1,0:T(8,128)} %obj_hbm.1, f32[2,128,128]{2,1,0:T(8,128)} %probe_hbm.1, f32[512,128]{1,0:T(8,128)} %bitcast.5, bf16[2,4,256,256]{3,2,1,0:T(8,128)(2,1)} %constant.2.clone.tab_hbm), custom_call_target="tpu_custom_call" | custom-call | tf_op jit(solution)/shard_map/step/pallas_call | solution.py:489
  79.8 1.3 %copy.10 = f32[4,2,256,256]{3,2,1,0:T(8,128)} copy(f32[4,2,256,256]{3,2,1,0:T(8,128)S(1)} %get-tuple-element.4) | data formatting | bytes 4194304
  81.1 0.7 copy.11
